TPU v7x, 32 devices: a whole 2x2x4 slice. The times are simulated.
32 devices in a mesh: walk: 8 (over z, x), chol: 4 (over y, core).
Axes of the slice: x: 2, y: 2, z: 4, core: 2. Of those that a mesh axis runs over, the one named last changes fastest.
Arguments:
- orbitals: bfloat16 [8, 400, 2048], P('walk', None, 'chol'), may hold values from -4 to 4
- intersection_inv: bfloat16 [8, 400, 400], P('walk'), may hold values from -0.18 to 0.18
- interp: bfloat16 [2048, 2048], P(None, 'chol'), may hold values from -0.079549513 to 0.079549513
- occ_interp: bfloat16 [400, 2048], P(None, 'chol'), may hold values from -0.18 to 0.18
- chol_factors: bfloat16 [2048, 2048], P('chol', 'walk'), may hold values from -2 to 2
- fields: float32 [8, 2048], P(None, 'walk'), may hold values from -4 to 4
Outputs:
- new_orbitals: bfloat16 [8, 400, 2048], P('walk', None, 'chol')
- force_bias: float32 [8, 2048], P(None, 'walk')
All inputs are finite; a program needn't handle non-finite values.
Results may differ from a plain program's by a relative error of at most 0.017.
Values may be sent and summed in bfloat16 or wider, within the bound.
A program may use at most 64 MiB of HBM per device.

v0:
```python
import jax
import jax.numpy as jnp
from jax import lax
from jax.sharding import PartitionSpec as P

TERMS = 4


time_root = 2.2


def on_device(orbitals, intersection_inv, interp, occ_interp, chol_factors, fields):
    walkers_here, electrons, basis_here = orbitals.shape
    piece = lax.all_gather(orbitals, "chol", axis=2, tiled=True)
    green = jnp.einsum(
        "wij,wjm->wim", intersection_inv, piece, preferred_element_type=jnp.float32
    ).astype(jnp.bfloat16)
    projected = jnp.einsum("wim,mp->wip", green, interp, preferred_element_type=jnp.float32)
    applied = jnp.einsum("wim,mp->wip", piece, interp, preferred_element_type=jnp.float32)
    projected, current = (projected, applied)
    weights = jnp.sum(occ_interp.astype(jnp.float32)[None] * projected, axis=1)
    factors = chol_factors.astype(jnp.float32)
    all_weights = lax.all_gather(weights, "walk", axis=0, tiled=True)
    partial_bias = jnp.dot(all_weights, factors, precision=lax.Precision.HIGHEST)
    force_bias = lax.psum(partial_bias, "chol")
    coeff = time_root * (fields - force_bias)
    field_part = jnp.dot(coeff, factors.T, precision=lax.Precision.HIGHEST)
    scales = lax.psum_scatter(field_part, "walk", scatter_dimension=0, tiled=True)
    total = orbitals.astype(jnp.float32)
    for order in range(1, TERMS + 1):
        mixed = (current * scales[:, None, :] / order).astype(jnp.bfloat16)
        partial_value = jnp.einsum("wnp,mp->wnm", mixed, interp, preferred_element_type=jnp.float32)
        term_whole = lax.psum(partial_value.astype(jnp.bfloat16), "chol")
        offset = lax.axis_index("chol") * basis_here
        term_local = lax.dynamic_slice_in_dim(term_whole, offset, basis_here, 2)
        total = total + term_local.astype(jnp.float32)
        if order < TERMS:
            current = jnp.einsum(
                "wnm,mp->wnp", term_whole, interp, preferred_element_type=jnp.float32
            )
    return (total.astype(jnp.bfloat16), force_bias)


def solution(mesh):
    placed = (
        P("walk", None, "chol"),
        P("walk", None, None),
        P(None, "chol"),
        P(None, "chol"),
        P("chol", "walk"),
        P(None, "walk"),
    )
    return jax.shard_map(
        on_device,
        mesh=mesh,
        in_specs=placed,
        out_specs=(P("walk", None, "chol"), P(None, "walk")),
        check_vma=False,
    )
```

profile of v0, /device:TPU:0, one launch (start us, length us, event | category | flops | bytes accessed | tf_op | source)
XLA Modules:
  0.0 304.3 jit_solution(10062563972776809825)
XLA Ops:
  7.2 0.0 all-gather.4.cloned.1.call-start
  7.2 0.7 all-gather.4.cloned.1.call-update
  7.9 0.0 all-reduce.6.cloned.1.call-start
  8.0 1.2 dynamic-slice
  9.2 23.1 %all-gather.4.cloned.1.call-done = bf16[1,400,2048]{2,1,0:T(8,128)(2,1)} async-done(((bf16[1,400,512]{2,1,0:T(8,128)(2,1)}), bf16[1,400,2048]{2,1,0:T(8,128)(2,1)}) %all-gather.4.cloned.1.call-update) | async-done | bytes 1638416 | tf_op jit(solution)/shard_map/all_gather | solution.py:14
  32.3 3.5 %fusion.46 = f32[512]{0:T(512)S(1)} fusion(bf16[2048,512]{1,0:T(8,128)(2,1)S(1)} %copy-done, bf16[1,400,2048]{2,1,0:T(8,128)(2,1)} %all-gather.4.cloned.1.call-done, bf16[400,512]{1,0:T(8,128)(2,1)} %param.9, bf16[1,400,400]{2,1,0:T(8,128)(2,1)} %param.7), kind=kOutput, calls=%fused_computation.30 | convolution fusion | flops 1495653888 | bytes 4467200 | tf_op jit(solution)/shard_map/wim,mp->wip/dot_general | solution.py:18
  35.8 26.2 %all-gather.1 = f32[8,1,512]{2,1,0:T(1,128)S(1)} all-gather(f32[1,1,512]{2,1,0:T(1,128)S(1)} %bitcast.75), channel_id=2, replica_groups=mesh['walk'=8,'chol'=4] {'walk'}, dimensions={0}, use_global_device_ids=true | all-gather | bytes 18432 | tf_op jit(solution)/shard_map/all_gather | solution.py:23
  62.0 0.2 fusion.66
  62.2 6.1 %psum.35 = f32[8,256]{1,0:T(8,128)S(1)} all-reduce(f32[8,256]{1,0:T(8,128)S(1)} %fusion.66), channel_id=1, replica_groups=mesh['walk'=8,'chol'=4] {'chol'}, use_global_device_ids=true, to_apply=%region_1.0 | all-reduce | flops 2048 | bytes 16384 | tf_op jit(solution)/shard_map/psum | solution.py:25
  68.3 0.3 fusion.69
  68.6 35.5 %all-reduce = f32[8,512]{1,0:T(8,128)S(1)} all-reduce(f32[8,512]{1,0:T(8,128)S(1)} %fusion.69), channel_id=3, replica_groups=mesh['walk'=8,'chol'=4] {'walk'}, use_global_device_ids=true, to_apply=%region_2.0.clone | all-reduce | flops 4096 | bytes 32768
  104.1 0.6 constant_dynamic-slice_fusion
  104.8 4.5 %fusion = bf16[1,400,2048]{2,1,0:T(8,128)(2,1)} fusion(bf16[2048,512]{1,0:T(8,128)(2,1)S(1)} %copy-done, bf16[1,400,2048]{2,1,0:T(8,128)(2,1)} %all-gather.4.cloned.1.call-done, f32[512]{0:T(512)S(1)} %bitcast.76), kind=kOutput, calls=%fused_computation.5 | convolution fusion | flops 1678950400 | bytes 5376000 | tf_op jit(solution)/shard_map/wnp,mp->wnm/dot_general | solution.py:32
  109.3 0.0 all-reduce.8.cloned.1.call-start
  109.4 40.0 %all-reduce.6.cloned.1.call-done = bf16[1,400,2048]{2,1,0:T(8,128)(2,1)} async-done(((bf16[1,400,2048]{2,1,0:T(8,128)(2,1)}), bf16[1,400,2048]{2,1,0:T(8,128)(2,1)}) %all-reduce.6.cloned.1.call-update) | async-done | bytes 1638416 | tf_op jit(solution)/shard_map/psum | solution.py:33
  149.4 4.5 %fusion.1 = bf16[1,400,2048]{2,1,0:T(8,128)(2,1)} fusion(bf16[2048,512]{1,0:T(8,128)(2,1)S(1)} %copy-done, bf16[1,400,2048]{2,1,0:T(8,128)(2,1)} %all-reduce.6.cloned.1.call-done, f32[512]{0:T(512)S(1)} %bitcast.77), kind=kOutput, calls=%fused_computation.6 | convolution fusion | flops 1679155200 | bytes 5376000 | tf_op jit(solution)/shard_map/wnp,mp->wnm/dot_general | solution.py:32
  153.9 0.0 all-reduce.10.cloned.1.call-start
  154.0 44.1 %all-reduce.8.cloned.1.call-done = bf16[1,400,2048]{2,1,0:T(8,128)(2,1)} async-done(((bf16[1,400,2048]{2,1,0:T(8,128)(2,1)}), bf16[1,400,2048]{2,1,0:T(8,128)(2,1)}) %all-reduce.8.cloned.1.call-update) | async-done | bytes 1638416 | tf_op jit(solution)/shard_map/psum | solution.py:33
  198.0 4.5 %fusion.2 = bf16[1,400,2048]{2,1,0:T(8,128)(2,1)} fusion(bf16[2048,512]{1,0:T(8,128)(2,1)S(1)} %copy-done, bf16[1,400,2048]{2,1,0:T(8,128)(2,1)} %all-reduce.8.cloned.1.call-done, f32[512]{0:T(512)S(1)} %bitcast.78), kind=kOutput, calls=%fused_computation.7 | convolution fusion | flops 1679155200 | bytes 5376000 | tf_op jit(solution)/shard_map/wnp,mp->wnm/dot_general | solution.py:32
  202.6 0.0 all-reduce.12.cloned.1.call-start
  202.6 44.1 %all-reduce.10.cloned.1.call-done = bf16[1,400,2048]{2,1,0:T(8,128)(2,1)} async-done(((bf16[1,400,2048]{2,1,0:T(8,128)(2,1)}), bf16[1,400,2048]{2,1,0:T(8,128)(2,1)}) %all-reduce.10.cloned.1.call-update) | async-done | bytes 1638416 | tf_op jit(solution)/shard_map/psum | solution.py:33
  246.7 4.5 %fusion.3 = bf16[1,400,2048]{2,1,0:T(8,128)(2,1)} fusion(bf16[2048,512]{1,0:T(8,128)(2,1)S(1)} %copy-done, bf16[1,400,2048]{2,1,0:T(8,128)(2,1)} %all-reduce.10.cloned.1.call-done, f32[512]{0:T(512)S(1)} %bitcast.79), kind=kOutput, calls=%fused_computation.8 | convolution fusion | flops 1679155200 | bytes 5376000 | tf_op jit(solution)/shard_map/wnp,mp->wnm/dot_general | solution.py:32
  251.3 44.1 %all-reduce.12.cloned.1.call-done = bf16[1,400,2048]{2,1,0:T(8,128)(2,1)} async-done(((bf16[1,400,2048]{2,1,0:T(8,128)(2,1)}), bf16[1,400,2048]{2,1,0:T(8,128)(2,1)}) %all-reduce.12.cloned.1.call-update) | async-done | bytes 1638416 | tf_op jit(solution)/shard_map/psum | solution.py:33
  295.4 2.4 add_convert_fusion
  (14 shorter events, 0.1 us)
Async XLA Ops:
  7.2 25.1 %copy-start = (bf16[2048,512]{1,0:T(8,128)(2,1)S(1)}, bf16[2048,512]{1,0:T(8,128)(2,1)}, u32[]{:S(2)}) copy-start(bf16[2048,512]{1,0:T(8,128)(2,1)} %param.8) | copy-start | bytes 6291460
  7.2 25.1 %all-gather.4.cloned.1.call-start = ((), (), s32[]{:S(2)}) async-start(), calls=%async_computation | async-start | bytes 2048000 | tf_op jit(solution)/shard_map/all_gather | solution.py:14
  7.9 141.5 %all-reduce.6.cloned.1.call-start = ((), (), s32[]{:S(2)}) async-start(), calls=%async_computation.1 | async-start | bytes 3276800 | tf_op jit(solution)/shard_map/psum | solution.py:33
  9.2 52.8 %copy-start.2 = (bf16[512,256]{1,0:T(8,128)(2,1)S(1)}, bf16[512,256]{1,0:T(8,128)(2,1)}, u32[]{:S(2)}) copy-start(bf16[512,256]{1,0:T(8,128)(2,1)} %param.10) | copy-start | bytes 786436
  9.2 59.1 %copy-start.4 = (f32[8,256]{1,0:T(8,128)S(1)}, f32[8,256]{1,0:T(8,128)}, u32[]{:S(2)}) copy-start(f32[8,256]{1,0:T(8,128)} %param.11) | copy-start | bytes 24580
  68.3 41.0 %copy-start.3 = (f32[8,256]{1,0:T(8,128)}, f32[8,256]{1,0:T(8,128)S(1)}, u32[]{:S(2)}) copy-start(f32[8,256]{1,0:T(8,128)S(1)} %psum.35) | copy-start | bytes 24580
  109.3 88.7 %all-reduce.8.cloned.1.call-start = ((), (), s32[]{:S(2)}) async-start(), calls=%async_computation.2 | async-start | bytes 3276800 | tf_op jit(solution)/shard_map/psum | solution.py:33
  153.9 92.8 %all-reduce.10.cloned.1.call-start = ((), (), s32[]{:S(2)}) async-start(), calls=%async_computation.3 | async-start | bytes 3276800 | tf_op jit(solution)/shard_map/psum | solution.py:33
  202.6 92.8 %all-reduce.12.cloned.1.call-start = ((), (), s32[]{:S(2)}) async-start(), calls=%async_computation.4 | async-start | bytes 3276800 | tf_op jit(solution)/shard_map/psum | solution.py:33
  251.2 44.2 %copy-start.1 = (bf16[1,400,512]{2,1,0:T(8,128)(2,1)S(1)}, bf16[1,400,512]{2,1,0:T(8,128)(2,1)}, u32[]{:S(2)}) copy-start(bf16[1,400,512]{2,1,0:T(8,128)(2,1)} %param.6) | copy-start | bytes 1228804
Sparse Core Ops, SparseCore 0:
  9.5 22.7 all-gather.3
  109.4 39.9 all-reduce.5
  154.0 43.9 all-reduce.7
  202.7 43.9 all-reduce.9
  251.4 43.9 all-reduce.11
where the time goes:
time: 305 us; the launch traced here: 304 us
  waiting for transfers between devices  196 us (64%)
  blocking collectives  67.8 us (22%)
  matrix products  22 us (7%)
  between operations  13.8 us (5%)
    psum x4, waiting for transfers between devices, on_device(): term_whole = lax.psum(partial_value.astype(jnp.bfloat16), 'chol')  172 us
    unnamed x1, blocking collectives  35.5 us
    all_gather x1, blocking collectives, on_device(): all_weights = lax.all_gather(weights, 'walk', axis=0, tiled=True)  26.2 us
    all_gather x1, waiting for transfers between devices, on_device(): piece = lax.all_gather(orbitals, 'chol', axis=2, tiled=True)  23.1 us
    dot_general x4, matrix products, on_device(): jnp.einsum('wnp,mp->wnm', mixed, interp, preferred_element_type=jnp.float32)  18 us
    psum x1, blocking collectives, on_device(): force_bias = lax.psum(partial_bias, 'chol')  6.12 us
  transfers between devices with their start and end apart: 5, of which 5 were waited for; matrix products, arithmetic and copies ran while one was open for 0% of the time, Pallas kernels for 0%

commit v1 on v0

v1 whole, which is shorter than its diff:
```python
import functools

import jax
import jax.numpy as jnp
from jax import lax
from jax.experimental import pallas as pl
from jax.experimental.pallas import tpu as pltpu
from jax.sharding import PartitionSpec as P

TERMS = 4
TILE = 16
CHUNKS = 4
EARLY = 1
MESH = pl.DeviceIdType.MESH

time_root = 2.2


def split_dot(a, b, dims):
    high = a.astype(jnp.bfloat16)
    rest = a - high.astype(jnp.float32)
    middle = rest.astype(jnp.bfloat16)
    low = (rest - middle.astype(jnp.float32)).astype(jnp.bfloat16)
    dot = functools.partial(
        lax.dot_general, dimension_numbers=(dims, ((), ())), preferred_element_type=jnp.float32
    )
    return dot(high, b) + (dot(middle, b) + dot(low, b))


def kernel(
    nw, nc, stride,
    orb, inv, interp, occ, fac, fld,
    out, bias_out,
    full, orbs, invv, occv, facv, fldv, term, acc, total, outb,
    wrow, allw, wmat, bpart, frow, crow, scal,
    loc, osib, oy, ofw, ysem, p1, p2, p3, sibo, sibs, asem, bsem, csem, dsem, esem,
):
    me_w = lax.axis_index("walk")
    me_c = lax.axis_index("chol")
    ny = nc // 2
    core = lax.rem(me_c, 2)
    y = me_c // 2
    sib = me_c + 1 - 2 * core
    basis, pts = interp.shape
    rows = orb.shape[0]
    own = (rows // TILE) // nc * TILE
    tail = rows - own * nc
    piece = basis // 4
    size = piece // CHUNKS

    bit_x = lax.rem(me_w, 2)
    bit_z = lax.rem(me_w // stride, 2)
    w_x = me_w + 1 - 2 * bit_x
    w_z = me_w + stride * (1 - 2 * bit_z)
    w_1 = w_x + core * (w_z - w_x)
    w_2 = w_z + core * (w_x - w_z)
    j_0 = 2 * bit_z + bit_x
    j_x = 2 * bit_z + 1 - bit_x
    j_z = 2 * (1 - bit_z) + bit_x
    j_1 = j_x + core * (j_z - j_x)
    j_2 = j_z + core * (j_x - j_z)
    pieces = (j_0, j_1, j_2, 3 - j_0)

    def send(src, dst, sems, index, w, c):
        return pltpu.make_async_remote_copy(
            src_ref=src, dst_ref=dst, send_sem=sems.at[(0,) + index], recv_sem=sems.at[(1,) + index],
            device_id=(w, c), device_id_type=MESH,
        )

    def chunk(stage, q):
        return pl.ds(pl.multiple_of(pieces[stage] * piece + q * size, size), size)

    def walk_peer(d):
        return lax.rem(me_w + d, nw)

    def chol_peer(d):
        return lax.rem(me_c + d, nc)

    local = [
        pltpu.make_async_copy(src, dst, loc.at[n])
        for n, (src, dst) in enumerate((
            (interp, full.at[me_c]), (orb, orbs.at[me_c]), (inv, invv), (occ, occv), (fac, facv), (fld, fldv),
        ))
    ]
    for copy in local:
        copy.start()

    barrier = pltpu.get_barrier_semaphore()
    for d in range(1, nw):
        pl.semaphore_signal(barrier, inc=1, device_id=(walk_peer(d), me_c), device_id_type=MESH)
    for d in range(1, nc):
        pl.semaphore_signal(barrier, inc=1, device_id=(me_w, chol_peer(d)), device_id_type=MESH)
    pl.semaphore_wait(barrier, nw + nc - 2)

    pending = []

    def go(copy):
        copy.start()
        pending.append(copy)
        return copy

    y_copies = {}

    def start_y(q):
        for d in range(1, ny):
            target = lax.rem(y + d, ny) * 2 + core
            at = chunk(0, q)
            y_copies[d, q] = go(send(interp.at[at], full.at[me_c, at], ysem, (d - 1, q), me_w, target))

    for q in range(EARLY):
        start_y(q)
    half = (rows // TILE + 1) // 2 * TILE
    parts = (pl.ds(0, half), pl.ds(half, rows - half))
    orb_y = {}
    for h, part in enumerate(parts):
        for d in range(1, ny):
            target = lax.rem(y + d, ny) * 2 + core
            orb_y[d, h] = go(send(orb.at[part], orbs.at[me_c, part], oy, (d - 1, h), me_w, target))
    orb_sib = go(send(orb, orbs.at[me_c], osib, (0,), me_w, sib))
    for q in range(EARLY, CHUNKS):
        start_y(q)
    own_sib = go(send(interp, full.at[me_c], sibo, (0,), me_w, sib))

    sib_copies = []

    def to_sibling(d, stage, q, block, at):
        copy = go(send(full.at[block, at], full.at[block, at], sibs, (d - 1, stage, q), me_w, sib))
        sib_copies.append(copy)

    first, second, third = {}, {}, {}

    def forward(stage, q):
        for d in range(1, ny):
            block = lax.rem(y - d + ny, ny) * 2 + core
            at = chunk(stage, q)
            place = full.at[block, at]
            if stage == 0:
                y_copies[d, q].wait_recv()
                first[d, q] = go(send(place, place, p1, (d - 1, q), w_1, me_c))
                second[d, q] = go(send(place, place, p2, (d - 1, q), w_2, me_c))
            elif stage == 1:
                first[d, q].wait_recv()
                third[d, q] = go(send(place, place, p3, (d - 1, q), w_2, me_c))
            elif stage == 2:
                second[d, q].wait_recv()
            else:
                third[d, q].wait_recv()
            to_sibling(d, stage, q, block, at)

    for q in range(EARLY):
        forward(0, q)

    orb_fw = []
    for h, part in enumerate(parts):
        for d in range(1, ny):
            block = lax.rem(y - d + ny, ny) * 2 + core
            orb_y[d, h].wait_recv()
            place = orbs.at[block, part]
            orb_fw.append(go(send(place, place, ofw, (d - 1, h), me_w, sib)))
    for copy in local:
        copy.wait()
    orb_sib.wait_recv()
    for copy in orb_fw:
        copy.wait_recv()

    applied = jnp.zeros((rows, pts), jnp.float32)
    depth = orb.shape[1]
    for c in range(nc):
        applied += jnp.dot(
            orbs[c], full[me_c, c * depth:(c + 1) * depth, :], preferred_element_type=jnp.float32
        )
    projected = jnp.dot(invv[...], applied.astype(jnp.bfloat16), preferred_element_type=jnp.float32)
    wrow[0] = jnp.sum(occv[...].astype(jnp.float32) * projected, axis=0, keepdims=True)
    allw[pl.ds(me_w, 1)] = wrow[...]
    a_copies = [
        go(send(wrow.at[0], allw.at[me_w], asem, (d - 1,), walk_peer(d), me_c)) for d in range(1, nw)
    ]

    for q in range(EARLY):
        forward(1, q)
        forward(2, q)
    forward(0, EARLY)

    for copy in a_copies:
        copy.wait_recv()
    for w in range(nw):
        wmat[w:w + 1, :] = allw[w]
    bpart[pl.ds(me_c, 1)] = split_dot(wmat[...], facv[...], ((1,), (0,)))[None]
    b_copies = [
        go(send(bpart.at[me_c], bpart.at[me_c], bsem, (d - 1,), me_w, chol_peer(d))) for d in range(1, nc)
    ]

    forward(0, EARLY + 1)
    for copy in b_copies:
        copy.wait_recv()
    bias = bpart[0]
    for c in range(1, nc):
        bias = bias + bpart[c]
    bias_out[...] = bias
    coeff = time_root * (fldv[...] - bias)
    part_scales = split_dot(coeff, facv[...], ((1,), (1,)))
    for w in range(nw):
        frow[w] = part_scales[w:w + 1, :]
    crow[pl.ds(me_w, 1)] = frow[pl.ds(me_w, 1)]
    c_copies = [
        go(send(frow.at[walk_peer(d)], crow.at[me_w], csem, (d - 1,), walk_peer(d), me_c))
        for d in range(1, nw)
    ]

    for q in range(EARLY, CHUNKS):
        if q > EARLY + 1:
            forward(0, q)
        forward(1, q)
        forward(2, q)
    for q in range(CHUNKS):
        forward(3, q)

    for copy in c_copies:
        copy.wait_recv()
    row = crow[0]
    for w in range(1, nw):
        row = row + crow[w]
    scal[pl.ds(me_c, 1)] = row[None]
    d_copies = [
        go(send(scal.at[me_c], scal.at[me_c], dsem, (d - 1,), me_w, chol_peer(d))) for d in range(1, nc)
    ]

    start = pl.multiple_of(me_c * own, TILE)
    for c in range(nc):
        columns = slice(c * depth, (c + 1) * depth)
        term[0:own, columns] = orbs[c, pl.ds(start, own), :]
        if tail:
            term[own:own + tail, columns] = orbs[c, own * nc:rows, :]
    total[...] = term[...].astype(jnp.float32)

    own_sib.wait_recv()
    for copy in d_copies:
        copy.wait_recv()
    for copy in sib_copies:
        copy.wait_recv()

    def taylor(order, carry):
        acc[...] = jnp.zeros_like(acc)
        inverse = 1.0 / (order + 1).astype(jnp.float32)

        def block(pb, carry):
            value = jnp.dot(term[...], full[pb], preferred_element_type=jnp.float32)
            mixed = (value * (scal[pb] * inverse)).astype(jnp.bfloat16)
            acc[...] += lax.dot_general(
                mixed, full[pb], (((1,), (1,)), ((), ())), preferred_element_type=jnp.float32
            )
            return carry

        lax.fori_loop(0, nc, block, 0)
        rounded = acc[...].astype(jnp.bfloat16)
        term[...] = rounded
        total[...] += rounded.astype(jnp.float32)
        return carry

    lax.fori_loop(0, TERMS, taylor, 0)

    for c in range(nc):
        outb[c] = total[:, c * depth:(c + 1) * depth].astype(jnp.bfloat16)
    mine = pl.ds(start, own)
    e_copies = [
        go(send(outb.at[chol_peer(d), 0:own], out.at[mine], esem, (d - 1,), me_w, chol_peer(d)))
        for d in range(1, nc)
    ]
    out[mine, :] = outb[me_c, 0:own, :]
    if tail:
        out[own * nc:rows, :] = outb[me_c, own:own + tail, :]
    for copy in e_copies:
        copy.wait_recv()
    for copy in pending:
        copy.wait_send()


def solution(mesh):
    nw, nc = mesh.shape["walk"], mesh.shape["chol"]
    stride = 2 ** ((nw.bit_length() - 1) // 2)

    def on_device(orbitals, intersection_inv, interp, occ_interp, chol_factors, fields):
        _, rows, depth = orbitals.shape
        basis, pts = interp.shape
        vecs = chol_factors.shape[1]
        ny = nc // 2
        links = max(ny - 1, 1)
        own = (rows // TILE) // nc * TILE
        held = own + rows - own * nc
        f32, bf16 = jnp.float32, jnp.bfloat16
        dma = pltpu.SemaphoreType.DMA
        anywhere = pl.BlockSpec(memory_space=pl.ANY)
        vmem = pl.BlockSpec(memory_space=pltpu.VMEM)
        new, bias = pl.pallas_call(
            functools.partial(kernel, nw, nc, stride),
            out_shape=(
                jax.ShapeDtypeStruct((rows, depth), bf16),
                jax.ShapeDtypeStruct((nw, vecs), f32),
            ),
            in_specs=[anywhere] * 6,
            out_specs=(vmem, vmem),
            scratch_shapes=[
                pltpu.VMEM((nc, basis, pts), bf16),
                pltpu.VMEM((nc, rows, depth), bf16),
                pltpu.VMEM((rows, rows), bf16),
                pltpu.VMEM((rows, pts), bf16),
                pltpu.VMEM((pts, vecs), bf16),
                pltpu.VMEM((nw, vecs), f32),
                pltpu.VMEM((held, basis), bf16),
                pltpu.VMEM((held, basis), f32),
                pltpu.VMEM((held, basis), f32),
                pltpu.VMEM((nc, held, depth), bf16),
                pltpu.VMEM((1, 1, pts), f32),
                pltpu.VMEM((nw, 1, pts), f32),
                pltpu.VMEM((nw, pts), f32),
                pltpu.VMEM((nc, nw, vecs), f32),
                pltpu.VMEM((nw, 1, pts), f32),
                pltpu.VMEM((nw, 1, pts), f32),
                pltpu.VMEM((nc, 1, pts), f32),
                dma((6,)),
                dma((2, 1)),
                dma((2, links, 2)),
                dma((2, links, 2)),
                dma((2, links, CHUNKS)),
                dma((2, links, CHUNKS)),
                dma((2, links, CHUNKS)),
                dma((2, links, CHUNKS)),
                dma((2, 1)),
                dma((2, links, 4, CHUNKS)),
                dma((2, nw - 1)),
                dma((2, nc - 1)),
                dma((2, nw - 1)),
                dma((2, nc - 1)),
                dma((2, nc - 1)),
            ],
            compiler_params=pltpu.CompilerParams(
                collective_id=0, has_side_effects=True, vmem_limit_bytes=60 * 2**20
            ),
        )(orbitals[0], intersection_inv[0], interp, occ_interp, chol_factors, fields)
        return new[None], bias

    placed = (
        P("walk", None, "chol"),
        P("walk", None, None),
        P(None, "chol"),
        P(None, "chol"),
        P("chol", "walk"),
        P(None, "walk"),
    )
    return jax.shard_map(
        on_device,
        mesh=mesh,
        in_specs=placed,
        out_specs=(P("walk", None, "chol"), P(None, "walk")),
        check_vma=False,
    )
```

time: 305 us -> 74.5 us (0.24)
  waiting for transfers between devices: 196 us -> 0 us
  Pallas kernels: 0 us -> 69.7 us
  blocking collectives: 67.8 us -> 0 us
  matrix products: 22 us -> 0 us
  between operations: 13.8 us -> 0.64 us
    psum x4 -> x0, waiting for transfers between devices: 172 us -> none  [on_device(): term_whole = lax.psum(partial_value.astype(jnp.bfloat16), 'chol')]
    pallas_call x0 -> x1, Pallas kernels: none -> 69.7 us  [on_device(): pl.pallas_call(functools.partial(kernel, nw, nc, stride), out_shape=(jax....]
    unnamed x1 -> x0, blocking collectives: 35.5 us -> none
    all_gather x1 -> x0, blocking collectives: 26.2 us -> none  [on_device(): all_weights = lax.all_gather(weights, 'walk', axis=0, tiled=True)]
    all_gather x1 -> x0, waiting for transfers between devices: 23.1 us -> none  [on_device(): piece = lax.all_gather(orbitals, 'chol', axis=2, tiled=True)]
    dot_general x7 -> x0, matrix products: 22 us -> none  [the longest x4 18 us: on_device(): jnp.einsum('wnp,mp->wnm', mixed, interp, preferred_element_type=jnp.float32)]
    psum x1 -> x0, blocking collectives: 6.12 us -> none  [on_device(): force_bias = lax.psum(partial_bias, 'chol')]
  transfers between devices with their start and end apart: 5 -> 0, of which waited for: 5 -> 0; matrix products, arithmetic and copies ran while one was open for 0% -> 0% of each run, Pallas kernels for 0% -> 0%
where the time goes in v1:
time: 74.5 us; the launch traced here: 73.5 us
  Pallas kernels  69.7 us (94%)
  local copies, waits for them, and re-layouts  3.07 us (4%)
    pallas_call x1, Pallas kernels, on_device(): pl.pallas_call(functools.partial(kernel, nw, nc, stride), out_shape=(jax....  69.7 us
    unnamed x2, local copies, waits for them, and re-layouts  3.07 us

profile of v1, /device:TPU:0, one launch (start us, length us, event | category | flops | bytes accessed | tf_op | source)
XLA Modules:
  0.0 73.5 jit_solution(9536214731915389072)
XLA Ops:
  0.6 69.7 %shard_map.77 = (bf16[400,512]{1,0:T(8,128)(2,1)}, f32[8,256]{1,0:T(8,128)}) custom-call(bf16[400,512]{1,0:T(8,128)(2,1)} %bitcast.3, bf16[400,400]{1,0:T(8,128)(2,1)} %bitcast.4, bf16[2048,512]{1,0:T(8,128)(2,1)} %interp.1, bf16[400,512]{1,0:T(8,128)(2,1)} %occ.1, bf16[512,256]{1,0:T(8,128)(2,1)} %fac.1, f32[8,256]{1,0:T(8,128)} %fld.1), custom_call_target="tpu_custom_call" | custom-call | tf_op jit(solution)/shard_map/pallas_call | solution.py:294
  70.4 1.8 %copy.10 = bf16[1,400,512]{2,1,0:T(8,128)(2,1)} copy(bf16[1,400,512]{2,1,0:T(8,128)(2,1)} %bitcast.5) | data formatting | bytes 819200
  72.2 1.3 %copy.11 = f32[8,256]{1,0:T(8,128)} copy(f32[8,256]{1,0:T(8,128)} %get-tuple-element.9) | data formatting | bytes 16384

commit v2 on v1

--- a/solution.py
+++ b/solution.py
@@ -10,7 +10,9 @@
 TERMS = 4
 TILE = 16
 CHUNKS = 4
-EARLY = 1
+EARLY = 3
+LAG = 1
+CUTS = (9, 12, 13, 16)
 MESH = pl.DeviceIdType.MESH
 
 time_root = 2.2
@@ -31,7 +33,7 @@
     nw, nc, stride,
     orb, inv, interp, occ, fac, fld,
     out, bias_out,
-    full, orbs, invv, occv, facv, fldv, term, acc, total, outb,
+    full, flip, orbs, invv, occv, facv, fldv, term, value, mixed, total, outb,
     wrow, allw, wmat, bpart, frow, crow, scal,
     loc, osib, oy, ofw, ysem, p1, p2, p3, sibo, sibs, asem, bsem, csem, dsem, esem,
 ):
@@ -147,8 +149,19 @@
                 third[d, q].wait_recv()
             to_sibling(d, stage, q, block, at)
 
-    for q in range(EARLY):
-        forward(0, q)
+    steps = []
+    for t in range(CHUNKS + 2):
+        for stage, q in ((0, t), (1, t - 1), (2, t - 1), (3, t - 1 - LAG)):
+            if 0 <= q < CHUNKS:
+                steps.append((stage, q))
+    steps += [(3, q) for q in range(CHUNKS) if (3, q) not in steps]
+    steps.sort(key=lambda step: not (step[1] < EARLY and step[0] < 3))
+
+    def forward_until(count):
+        while steps and len(steps) > 4 * CHUNKS - count:
+            forward(*steps.pop(0))
+
+    forward_until(CUTS[0])
 
     orb_fw = []
     for h, part in enumerate(parts):
@@ -176,10 +189,10 @@
         go(send(wrow.at[0], allw.at[me_w], asem, (d - 1,), walk_peer(d), me_c)) for d in range(1, nw)
     ]
 
-    for q in range(EARLY):
-        forward(1, q)
-        forward(2, q)
-    forward(0, EARLY)
+    forward_until(CUTS[1])
+    for c in range(nc):
+        span = slice(c * depth, (c + 1) * depth)
+        flip[0, :, span] = full[me_c, span, :].T
 
     for copy in a_copies:
         copy.wait_recv()
@@ -190,7 +203,11 @@
         go(send(bpart.at[me_c], bpart.at[me_c], bsem, (d - 1,), me_w, chol_peer(d))) for d in range(1, nc)
     ]
 
-    forward(0, EARLY + 1)
+    forward_until(CUTS[2])
+    own_sib.wait_recv()
+    for c in range(nc):
+        span = slice(c * depth, (c + 1) * depth)
+        flip[1, :, span] = full[sib, span, :].T
     for copy in b_copies:
         copy.wait_recv()
     bias = bpart[0]
@@ -207,23 +224,7 @@
         for d in range(1, nw)
     ]
 
-    for q in range(EARLY, CHUNKS):
-        if q > EARLY + 1:
-            forward(0, q)
-        forward(1, q)
-        forward(2, q)
-    for q in range(CHUNKS):
-        forward(3, q)
-
-    for copy in c_copies:
-        copy.wait_recv()
-    row = crow[0]
-    for w in range(1, nw):
-        row = row + crow[w]
-    scal[pl.ds(me_c, 1)] = row[None]
-    d_copies = [
-        go(send(scal.at[me_c], scal.at[me_c], dsem, (d - 1,), me_w, chol_peer(d))) for d in range(1, nc)
-    ]
+    forward_until(CUTS[3])
 
     start = pl.multiple_of(me_c * own, TILE)
     for c in range(nc):
@@ -233,42 +234,77 @@
             term[own:own + tail, columns] = orbs[c, own * nc:rows, :]
     total[...] = term[...].astype(jnp.float32)
 
-    own_sib.wait_recv()
+    forward_until(4 * CHUNKS)
+    for copy in sib_copies:
+        copy.wait_recv()
+
+    def open_block(pb, carry):
+        value[pb] = jnp.dot(term[...], full[pb], preferred_element_type=jnp.float32)
+        return carry
+
+    lax.fori_loop(0, nc, open_block, 0)
+
+    for copy in c_copies:
+        copy.wait_recv()
+    row = crow[0]
+    for w in range(1, nw):
+        row = row + crow[w]
+    scal[pl.ds(me_c, 1)] = row[None]
+    d_copies = [
+        go(send(scal.at[me_c], scal.at[me_c], dsem, (d - 1,), me_w, chol_peer(d))) for d in range(1, nc)
+    ]
     for copy in d_copies:
         copy.wait_recv()
-    for copy in sib_copies:
-        copy.wait_recv()
+
+    def mix(pb, order):
+        mixed[pb] = (value[pb] * (scal[pb] * (1.0 / order))).astype(jnp.bfloat16)
+
+    def back(mb):
+        at = pl.ds(pl.multiple_of(mb * depth, depth), depth)
+        result = jnp.zeros((term.shape[0], depth), jnp.float32)
+        for n, pb in enumerate((me_c, sib)):
+            result += jnp.dot(mixed[pb], flip[n, :, at], preferred_element_type=jnp.float32)
+        for d, e in [(d, e) for d in range(1, ny) for e in (0, 1)]:
+            pb = lax.rem(y + d, ny) * 2 + e
+            result += lax.dot_general(
+                mixed[pb], full[pb, at, :], (((1,), (1,)), ((), ())), preferred_element_type=jnp.float32
+            )
+        rounded = result.astype(jnp.bfloat16)
+        term[:, at] = rounded
+        summed = total[:, at] + rounded.astype(jnp.float32)
+        total[:, at] = summed
+        return summed
+
+    for pb in range(nc):
+        mix(pb, jnp.float32(1.0))
 
     def taylor(order, carry):
-        acc[...] = jnp.zeros_like(acc)
-        inverse = 1.0 / (order + 1).astype(jnp.float32)
+        def back_block(mb, carry):
+            back(mb)
+            return carry
 
         def block(pb, carry):
-            value = jnp.dot(term[...], full[pb], preferred_element_type=jnp.float32)
-            mixed = (value * (scal[pb] * inverse)).astype(jnp.bfloat16)
-            acc[...] += lax.dot_general(
-                mixed, full[pb], (((1,), (1,)), ((), ())), preferred_element_type=jnp.float32
-            )
+            value[pb] = jnp.dot(term[...], full[pb], preferred_element_type=jnp.float32)
+            mix(pb, order.astype(jnp.float32))
             return carry
 
+        lax.fori_loop(0, nc, back_block, 0)
         lax.fori_loop(0, nc, block, 0)
-        rounded = acc[...].astype(jnp.bfloat16)
-        term[...] = rounded
-        total[...] += rounded.astype(jnp.float32)
         return carry
 
-    lax.fori_loop(0, TERMS, taylor, 0)
-
-    for c in range(nc):
-        outb[c] = total[:, c * depth:(c + 1) * depth].astype(jnp.bfloat16)
+    lax.fori_loop(2, TERMS + 1, taylor, 0)
+
     mine = pl.ds(start, own)
-    e_copies = [
-        go(send(outb.at[chol_peer(d), 0:own], out.at[mine], esem, (d - 1,), me_w, chol_peer(d)))
-        for d in range(1, nc)
-    ]
-    out[mine, :] = outb[me_c, 0:own, :]
+    e_copies = []
+    hops = [(d, e) for d in range(1, ny) for e in (0, 1)] + [(0, 1), (0, 0)]
+    for n, (d, e) in enumerate(hops):
+        c = lax.rem(y + d, ny) * 2 + (core if e == 0 else 1 - core)
+        outb[n] = back(c).astype(jnp.bfloat16)
+        if n < nc - 1:
+            e_copies.append(go(send(outb.at[n, 0:own], out.at[mine], esem, (n,), me_w, c)))
+    out[mine, :] = outb[nc - 1, 0:own, :]
     if tail:
-        out[own * nc:rows, :] = outb[me_c, own:own + tail, :]
+        out[own * nc:rows, :] = outb[nc - 1, own:own + tail, :]
     for copy in e_copies:
         copy.wait_recv()
     for copy in pending:
@@ -301,13 +337,15 @@
             out_specs=(vmem, vmem),
             scratch_shapes=[
                 pltpu.VMEM((nc, basis, pts), bf16),
+                pltpu.VMEM((2, pts, basis), bf16),
                 pltpu.VMEM((nc, rows, depth), bf16),
                 pltpu.VMEM((rows, rows), bf16),
                 pltpu.VMEM((rows, pts), bf16),
                 pltpu.VMEM((pts, vecs), bf16),
                 pltpu.VMEM((nw, vecs), f32),
                 pltpu.VMEM((held, basis), bf16),
-                pltpu.VMEM((held, basis), f32),
+                pltpu.VMEM((nc, held, pts), f32),
+                pltpu.VMEM((nc, held, pts), bf16),
                 pltpu.VMEM((held, basis), f32),
                 pltpu.VMEM((nc, held, depth), bf16),
                 pltpu.VMEM((1, 1, pts), f32),

time: 74.5 us -> 67.1 us (0.901); the launches traced: 73.5 us -> 66.9 us
  Pallas kernels: 69.7 us -> 63.2 us
    pallas_call x1, Pallas kernels: 69.7 us -> 63.2 us  [on_device(): pl.pallas_call(functools.partial(kernel, nw, nc, stride), out_shape=(jax....]
where the time goes in v2:
time: 67.1 us; the launch traced here: 66.9 us
  Pallas kernels  63.2 us (94%)
  local copies, waits for them, and re-layouts  3.07 us (5%)
    pallas_call x1, Pallas kernels, on_device(): pl.pallas_call(functools.partial(kernel, nw, nc, stride), out_shape=(jax....  63.2 us
    unnamed x2, local copies, waits for them, and re-layouts  3.07 us

profile of v2, /device:TPU:0, one launch (start us, length us, event | category | flops | bytes accessed | tf_op | source)
XLA Modules:
  0.0 66.9 jit_solution(9982223197401755375)
XLA Ops:
  0.6 63.2 %shard_map.77 = (bf16[400,512]{1,0:T(8,128)(2,1)}, f32[8,256]{1,0:T(8,128)}) custom-call(bf16[400,512]{1,0:T(8,128)(2,1)} %bitcast.3, bf16[400,400]{1,0:T(8,128)(2,1)} %bitcast.4, bf16[2048,512]{1,0:T(8,128)(2,1)} %interp.1, bf16[400,512]{1,0:T(8,128)(2,1)} %occ.1, bf16[512,256]{1,0:T(8,128)(2,1)} %fac.1, f32[8,256]{1,0:T(8,128)} %fld.1), custom_call_target="tpu_custom_call" | custom-call | tf_op jit(solution)/shard_map/pallas_call | solution.py:330
  63.8 1.8 %copy.10 = bf16[1,400,512]{2,1,0:T(8,128)(2,1)} copy(bf16[1,400,512]{2,1,0:T(8,128)(2,1)} %bitcast.5) | data formatting | bytes 819200
  65.6 1.3 %copy.11 = f32[8,256]{1,0:T(8,128)} copy(f32[8,256]{1,0:T(8,128)} %get-tuple-element.9) | data formatting | bytes 16384
